TPU v7x, 32 devices: a whole 2x2x4 slice. The times are simulated.
32 devices in a mesh: rows: 4 (over x, core), batch: 8 (over z, y).
Axes of the slice: x: 2, y: 2, z: 4, core: 2. Of those that a mesh axis runs over, the one named last changes fastest.
Arguments:
- features: bfloat16 [96, 8, 32, 512], P('batch', 'rows'), may hold values from -12 to 12
- norm_gain: float32 [512], replicated, may hold values from 0.25 to 1.75
- norm_bias: float32 [512], replicated, may hold values from -2.5 to 2.5
- conv_weight: bfloat16 [4, 4608], replicated, may hold values from -0.09375 to 0.09375
- embed_weight: float32 [16, 1024], replicated, may hold values from -1.5 to 1.5
- embed_bias: float32 [1024], replicated, may hold values from -2.5 to 2.5
- proj_in: bfloat16 [1024, 2048], P('rows'), may hold values from -0.1875 to 0.1875
- proj_in_bias: float32 [2048], replicated, may hold values from -2.5 to 2.5
- proj_out: bfloat16 [2048, 768], P('rows'), may hold values from -0.125 to 0.125
- proj_out_bias: float32 [768], replicated, may hold values from -2.5 to 2.5
- targets: bfloat16 [96, 4, 16, 768], P('batch', 'rows'), may hold values from -6 to 6
Outputs:
- grad_features: bfloat16 [96, 8, 32, 512], P('batch', 'rows')
- grad_conv: float32 [4, 4608], replicated
- grad_gain: float32 [512], replicated
- grad_bias: float32 [512], replicated
- grad_embed: float32 [16, 1024], replicated
All inputs are finite; a program needn't handle non-finite values.
Results may differ from a plain program's by a relative error of at most 0.012.
Values may be sent and summed in bfloat16 or wider, within the bound.
A program may use at most 128 MiB of HBM per device.

v0:
```python
import jax
import jax.numpy as jnp
from jax import lax
from jax.sharding import PartitionSpec as P

GROUPS = 32
LATENT = 4
PATCH = 2
ALIGN = 768
EPS_NORM = 1e-06
EPS_UNIT = 1e-06


def padded(block, sides, width):
    for axis, dim in sides:
        count = lax.axis_size(axis)
        forward = [(i, i + 1) for i in range(count - 1)]
        backward = [(target, source) for source, target in forward]
        low = lax.ppermute(
            lax.slice_in_dim(block, block.shape[dim] - width, None, axis=dim), axis, forward
        )
        high = lax.ppermute(lax.slice_in_dim(block, 0, width, axis=dim), axis, backward)
        block = jnp.concatenate([low, block, high], axis=dim)
    return block


def swish_slope(values):
    sig = jax.nn.sigmoid(values)
    return sig * (1.0 + values * (1.0 - sig))


def shards(
    features,
    norm_gain,
    norm_bias,
    conv_weight,
    embed_weight,
    embed_bias,
    proj_in,
    proj_in_bias,
    proj_out,
    proj_out_bias,
    targets,
):
    images, height, across, channels = features.shape
    per_group = channels // GROUPS
    members = lax.axis_size("rows") * height * across * per_group
    cell_count = images * height * across
    values = features.astype(jnp.float32)
    grouped = values.reshape(images, height * across, GROUPS, per_group)
    totals = lax.psum(jnp.sum(grouped, axis=(1, 3)), "rows")
    centred = grouped - (totals / members)[:, None, :, None]
    squares = lax.psum(jnp.sum(centred * centred, axis=(1, 3)), "rows")
    variance = squares / members
    inverse = lax.rsqrt(variance + EPS_NORM)[:, None, :, None]
    normed = (centred * inverse).reshape(images, height, across, channels)
    shifted = normed * norm_gain + norm_bias
    active = (shifted * jax.nn.sigmoid(shifted)).astype(jnp.bfloat16)
    active_flat = active.reshape(cell_count, channels)
    kernel_stack = (
        conv_weight.reshape(LATENT, 9, channels).transpose(2, 1, 0).reshape(channels, 9 * LATENT)
    )
    tap_terms = jnp.dot(active_flat, kernel_stack, preferred_element_type=jnp.float32)
    tap_terms = tap_terms.reshape(images, height, across, 9, LATENT)
    tap_pad = jnp.pad(tap_terms, ((0, 0), (2, 2), (1, 1), (0, 0), (0, 0)))
    extended = jnp.zeros((images, height + 2, across, LATENT), jnp.float32)
    for position in range(9):
        row_off, col_off = (position // 3, position % 3)
        extended = (
            extended
            + tap_pad[:, row_off : row_off + height + 2, col_off : col_off + across, position, :]
        )
    edges = jnp.concatenate([extended[:, 0:1], extended[:, height + 1 : height + 2]], axis=1)
    arrived = padded(edges, (("rows", 1),), 1)
    latent = extended[:, 1 : height + 1]
    latent = latent.at[:, 0].add(arrived[:, 0])
    latent = latent.at[:, height - 1].add(arrived[:, 3])
    tok_rows = height // PATCH
    tok_cols = across // PATCH
    tok_count = images * tok_rows * tok_cols
    patches = (
        latent.reshape(images, tok_rows, PATCH, tok_cols, PATCH, LATENT)
        .transpose(0, 1, 3, 2, 4, 5)
        .reshape(tok_count, PATCH * PATCH * LATENT)
    )
    embedded = (
        jnp.dot(patches, embed_weight, precision=lax.Precision.HIGHEST) + embed_bias
    ).astype(jnp.bfloat16)
    full_in, full_out = (
        lax.all_gather(proj_in, "rows", axis=0, tiled=True),
        lax.all_gather(proj_out, "rows", axis=0, tiled=True),
    )
    hidden_pre = jnp.dot(embedded, full_in, preferred_element_type=jnp.float32) + proj_in_bias
    hidden_act = (hidden_pre * jax.nn.sigmoid(hidden_pre)).astype(jnp.bfloat16)
    projected = jnp.dot(hidden_act, full_out, preferred_element_type=jnp.float32) + proj_out_bias
    target = targets.reshape(tok_count, ALIGN).astype(jnp.float32)
    unit_target = target * lax.rsqrt(jnp.sum(target * target, axis=1, keepdims=True) + EPS_UNIT)
    inv_len = lax.rsqrt(jnp.sum(projected * projected, axis=1, keepdims=True) + EPS_UNIT)
    unit_proj = projected * inv_len
    cosine = jnp.sum(unit_proj * unit_target, axis=1, keepdims=True)
    grad_out = (-inv_len * (unit_target - cosine * unit_proj)).astype(jnp.bfloat16)
    back_hidden = lax.dot_general(
        grad_out, full_out, (((1,), (1,)), ((), ())), preferred_element_type=jnp.float32
    )
    grad_hidden = (back_hidden * swish_slope(hidden_pre)).astype(jnp.bfloat16)
    grad_embedded = lax.dot_general(
        grad_hidden, full_in, (((1,), (1,)), ((), ())), preferred_element_type=jnp.float32
    )
    embed_part = lax.dot_general(
        patches, grad_embedded, (((0,), (0,)), ((), ())), precision=lax.Precision.HIGHEST
    )
    grad_patch = lax.dot_general(
        grad_embedded, embed_weight, (((1,), (1,)), ((), ())), precision=lax.Precision.HIGHEST
    )
    grad_latent = (
        grad_patch.reshape(images, tok_rows, tok_cols, PATCH, PATCH, LATENT)
        .transpose(0, 1, 3, 2, 4, 5)
        .reshape(images, height, across, LATENT)
        .astype(jnp.bfloat16)
    )
    grad_pad = padded(grad_latent, (("rows", 1),), 1)
    grad_pad = jnp.pad(grad_pad, ((0, 0), (0, 0), (1, 1), (0, 0)))
    shifted_grads = []
    for position in range(9):
        row_off, col_off = (position // 3, position % 3)
        shifted_grads.append(
            grad_pad[:, 2 - row_off : 2 - row_off + height, 2 - col_off : 2 - col_off + across, :]
        )
    grad_taps = jnp.concatenate(shifted_grads, axis=3).reshape(cell_count, 9 * LATENT)
    conv_stack = lax.dot_general(
        active_flat, grad_taps, (((0,), (0,)), ((), ())), preferred_element_type=jnp.float32
    )
    conv_part = (
        conv_stack.reshape(channels, 9, LATENT).transpose(2, 1, 0).reshape(LATENT, 9 * channels)
    )
    grad_active = lax.dot_general(
        grad_taps, kernel_stack, (((1,), (1,)), ((), ())), preferred_element_type=jnp.float32
    )
    flat_shift = shifted.reshape(cell_count, channels)
    flat_normed = normed.reshape(cell_count, channels)
    grad_shift = grad_active * swish_slope(flat_shift)
    gain_part = jnp.sum(grad_shift * flat_normed, axis=0)
    bias_part = jnp.sum(grad_shift, axis=0)
    grad_norm = (grad_shift * norm_gain).reshape(images, height * across, GROUPS, per_group)
    normed_groups = flat_normed.reshape(images, height * across, GROUPS, per_group)
    first, second = lax.psum(
        (jnp.sum(grad_norm, axis=(1, 3)), jnp.sum(grad_norm * normed_groups, axis=(1, 3))), "rows"
    )
    grad_values = inverse * (
        grad_norm
        - (first / members)[:, None, :, None]
        - normed_groups * (second / members)[:, None, :, None]
    )
    grad_features = grad_values.reshape(images, height, across, channels).astype(jnp.bfloat16)
    grad_conv, grad_gain, grad_bias, grad_embed = lax.psum(
        (conv_part, gain_part, bias_part, embed_part), ("rows", "batch")
    )
    return (grad_features, grad_conv, grad_gain, grad_bias, grad_embed)


def solution(mesh):
    in_specs = (
        P("batch", "rows", None, None),
        P(),
        P(),
        P(),
        P(),
        P(),
        P("rows", None),
        P(),
        P("rows", None),
        P(),
        P("batch", "rows", None, None),
    )
    out_specs = (P("batch", "rows", None, None), P(), P(), P(), P())
    return jax.shard_map(shards, mesh=mesh, in_specs=in_specs, out_specs=out_specs, check_vma=False)
```

profile of v0, /device:TPU:8, one launch (start us, length us, event | category | flops | bytes accessed | tf_op | source)
XLA Modules:
  0.0 264.1 jit_solution(803283353714649149)
XLA Ops:
  7.2 0.7 all-gather.3.cloned.1.call-update
  8.0 0.7 all-gather.5.cloned.1.call-update
  8.9 0.2 convert_reduce_fusion
  9.3 7.0 %psum.56 = f32[12,32]{1,0:T(8,128)S(1)} all-reduce(f32[12,32]{1,0:T(8,128)S(1)} %reduce_sum.97), channel_id=1, replica_groups=mesh['rows'=4,'batch'=8] {'rows'}, use_global_device_ids=true, to_apply=%region_2.0 | all-reduce | flops 384 | bytes 3072 | tf_op jit(solution)/shard_map/psum | solution.py:51
  16.5 0.1 sub.51
  16.6 0.2 multiply_reduce_fusion.1
  17.1 6.2 %psum.57 = f32[12,32]{1,0:T(8,128)S(1)} all-reduce(f32[12,32]{1,0:T(8,128)S(1)} %reduce_sum.100), channel_id=1, replica_groups=mesh['rows'=4,'batch'=8] {'rows'}, use_global_device_ids=true, to_apply=%region_5.6 | all-reduce | flops 384 | bytes 3072 | tf_op jit(solution)/shard_map/psum | solution.py:53
  23.5 0.1 mul.137
  23.6 1.7 multiply_convert_fusion.2
  25.3 0.8 fusion.12
  26.1 0.7 fusion.35
  26.8 0.6 fusion.47
  27.4 1.3 collective-permute-start.1
  28.7 3.6 %collective-permute-start = (f32[12,1,32,4]{2,3,1,0:T(4,128)}, f32[12,1,32,4]{2,3,1,0:T(4,128)}, u32[]{:S(2)}, u32[]{:S(2)}) collective-permute-start(f32[12,1,32,4]{2,3,1,0:T(4,128)} %get-tuple-element.43), channel_id=1, source_target_pairs={{0,8},{8,16},{16,24},{1,9},{9,17},{17,25},{2,10},{10,18},{18,26},{... | collective-permute-start | bytes 18440 | tf_op jit(solution)/shard_map/ppermute | solution.py:19
  32.3 0.1 multiply_reduce_fusion.3
  32.5 0.9 bitcast_multiply_fusion.1
  33.7 6.2 %copy.155 = f32[12,2,32,512]{2,1,0,3:T(2,128)} copy(bf16[12,2,32,512]{3,2,1,0:T(8,128)(2,1)S(1)} %copy-done.1) | data formatting | bytes 2359296 | tf_op jit(solution)/shard_map/reshape | solution.py:50
  39.9 2.4 mul.163
  42.3 3.4 %mul.171 = f32[768,512]{0,1:T(8,128)S(1)} reshape(f32[12,64,32,16]{1,0,3,2:T(8,128)} %mul.163) | data formatting | bytes 3145728 | tf_op jit(solution)/shard_map/mul | solution.py:149
  45.7 1.6 copy.150
  47.3 2.4 sub.61
  49.7 3.3 %sub.64 = f32[768,512]{0,1:T(8,128)S(1)} reshape(f32[12,64,32,16]{1,0,3,2:T(8,128)} %sub.61) | data formatting | bytes 3145728 | tf_op jit(solution)/shard_map/sub | solution.py:52
  53.1 1.6 copy.149
  54.7 7.8 %reshape.201 = f32[12,64,32,16]{1,0,3,2:T(8,128)} reshape(f32[12,2,32,512]{2,1,0,3:T(2,128)} %copy.155) | data formatting | bytes 3145728 | tf_op jit(solution)/shard_map/reshape | solution.py:50
  62.5 0.8 fusion.41
  63.4 0.2 copy.138
  63.7 0.8 fusion.10
  64.6 4.3 %convolution_add_fusion = f32[192,2048]{1,0:T(8,128)} fusion(bf16[192,1024]{1,0:T(8,128)(2,1)S(1)} %fusion.10, bf16[1024,2048]{1,0:T(8,128)(2,1)} %all-gather.3.cloned.1.call-done, f32[2048]{0:T(1024)S(1)} %copy-done.6), kind=kOutput, calls=%fused_computation.11 | convolution fusion | flops 805699584 | bytes 6168576 | tf_op jit(solution)/shard_map/dot_general | solution.py:93
  68.9 6.9 %all-gather.5.cloned.1.call-done = bf16[2048,768]{1,0:T(8,128)(2,1)} async-done(((bf16[512,768]{1,0:T(8,128)(2,1)}), bf16[2048,768]{1,0:T(8,128)(2,1)}) %all-gather.5.cloned.1.call-update) | async-done | bytes 3145744 | tf_op jit(solution)/shard_map/all_gather | solution.py:91
  75.8 3.4 %multiply_reduce_fusion.4 = (f32[192]{0:T(256)S(1)}, f32[192,768]{1,0:T(8,128)S(1)}) fusion(f32[768]{0:T(1024)S(1)} %copy-done.10, bf16[2048,768]{1,0:T(8,128)(2,1)} %all-gather.5.cloned.1.call-done, f32[192,2048]{1,0:T(8,128)} %convolution_add_fusion), kind=kOutput, calls=%fused_computation.47 | convolution fusion | flops 606388032 | bytes 5312256 | tf_op jit(solution)/shard_map/dot_general | solution.py:95
  79.3 0.2 multiply_reduce_fusion.2
  79.5 0.5 copy-done.4
  80.1 6.4 %fusion.11 = f32[192,1024]{1,0:T(8,128)S(1)} fusion(bf16[1024,2048]{1,0:T(8,128)(2,1)} %all-gather.3.cloned.1.call-done, bf16[2048,768]{1,0:T(8,128)(2,1)} %all-gather.5.cloned.1.call-done, f32[192,2048]{1,0:T(8,128)} %convolution_add_fusion, f32[192,768]{1,0:T(8,128)S(1)} %copy-done.2, f32[192,768]{1,0:T(8,128)} %copy-done.4, ...), kind=kOutput, calls=%fused_computation.37 | convolution fusion | flops 1413562368 | bytes 10881280 | tf_op jit(solution)/shard_map/dot_general | solution.py:106
  86.5 0.7 convolution_convert_fusion
  87.3 0.2 copy.139
  87.5 2.1 collective-permute-start.2
  89.7 1.5 collective-permute-start.3
  91.2 1.1 fusion.49
  92.3 0.5 collective-permute-done.3
  92.8 0.7 slice_dynamic-update-slice_fusion.5
  93.5 0.6 fusion.38
  94.1 0.6 slice_dynamic-update-slice_fusion.4
  94.8 0.7 slice_dynamic-update-slice_fusion.3
  95.4 0.6 constant_dynamic-update-slice_fusion
  96.1 0.6 slice_dynamic-update-slice_fusion.2
  96.7 0.7 slice_dynamic-update-slice_fusion.1
  97.4 0.6 fusion.37
  98.0 0.6 slice_dynamic-update-slice_fusion
  98.6 1.6 copy.140
  100.2 0.2 reshape.185
  100.4 0.3 convolution_bitcast_fusion
  100.7 0.7 copy.157
  101.4 3.3 %fusion.46 = (f32[512]{0:T(512)S(1)}, f32[512]{0:T(512)S(1)}, f32[768,512]{1,0:T(8,128)S(1)}) fusion(f32[768,512]{1,0:T(8,128)} %copy.150, f32[768,512]{1,0:T(8,128)} %copy.149, bf16[12,2,32,512]{3,2,1,0:T(8,128)(2,1)S(1)} %copy-done.1, f32[512]{0:T(512)S(1)} %copy-done.9, f32[12,2,32,512]{3,2,1,0:T(8,128)} %get-tuple-element.41, ...), kind=kOutput, calls=%fused_computation.94 | convolution fusion | flops 34208768 | bytes 7176192 | tf_op jit(solution)/shard_map/dot_general | solution.py:136
  104.7 1.6 copy.141
  106.3 4.0 %reshape.188 = f32[12,64,32,16]{1,0,3,2:T(8,128)} reshape(f32[768,512]{0,1:T(8,128)} %copy.141) | data formatting | bytes 3145728 | tf_op jit(solution)/shard_map/reshape | solution.py:144
  110.3 4.7 %fusion.45 = (f32[12,32]{0,1:T(8,128)S(1)}, f32[12,32]{0,1:T(8,128)S(1)}) fusion(f32[12,64,32,16]{1,0,3,2:T(8,128)} %reshape.188, f32[12,32]{0,1:T(8,128)S(1)} %copy.146, f32[12,64,32,16]{1,0,3,2:T(8,128)} %reshape.201, f32[12,32]{0,1:T(8,128)S(1)} %copy.144), kind=kLoop, calls=%fused_computation.93 | loop fusion | flops 1965312 | bytes 3151872 | tf_op jit(solution)/shard_map/reduce_sum | solution.py:147
  115.2 12.6 %all-reduce.4 = (f32[12,32]{1,0:T(8,128)S(1)}, f32[12,32]{1,0:T(8,128)S(1)}) all-reduce(f32[12,32]{1,0:T(8,128)S(1)} %copy.147, f32[12,32]{1,0:T(8,128)S(1)} %copy.142), channel_id=1, replica_groups=mesh['rows'=4,'batch'=8] {'rows'}, use_global_device_ids=true, to_apply=%region_12.13 | all-reduce | flops 768 | bytes 6144 | tf_op jit(solution)/shard_map/psum | solution.py:146
  127.9 0.1 mul.167
  128.1 0.1 sub.58
  128.3 1.3 multiply_convert_fusion
  129.6 40.3 %all-reduce.2 = (f32[512]{0:T(512)}, f32[512]{0:T(512)}) all-reduce(f32[512]{0:T(512)S(1)} %get-tuple-element.32, f32[512]{0:T(512)S(1)} %get-tuple-element.31), channel_id=1, replica_groups=mesh['rows'=4,'batch'=8] {'rows','batch'}, use_global_device_ids=true, to_apply=%region_15.16 | all-reduce | flops 1024 | bytes 8192 | tf_op jit(solution)/shard_map/psum | solution.py:155
  169.9 84.6 %all-reduce.7.cloned.1.call-done = (f32[4,4608]{1,0:T(4,128)}, f32[16,1024]{1,0:T(8,128)}) async-done(((f32[4,4608]{1,0:T(4,128)}, f32[16,1024]{1,0:T(8,128)}), (f32[4,4608]{1,0:T(4,128)}, f32[16,1024]{1,0:T(8,128)})) %all-reduce.7.cloned.1.call-update) | async-done | bytes 139280 | tf_op jit(solution)/shard_map/psum | solution.py:155
  254.5 1.5 copy.174
  256.1 1.5 copy.175
  (59 shorter events, 2.1 us)
Async XLA Ops:
  7.2 56.6 %copy-start = (f32[16,1024]{1,0:T(8,128)S(1)}, f32[16,1024]{1,0:T(8,128)}, u32[]{:S(2)}) copy-start(f32[16,1024]{1,0:T(8,128)} %param.19) | copy-start | bytes 196612
  7.2 1.6 copy-start.5
  7.2 1.7 copy-start.1
  7.2 57.4 %all-gather.3.cloned.1.call-start = ((), (), s32[]{:S(2)}) async-start(), calls=%async_computation | async-start | bytes 5242880 | tf_op jit(solution)/shard_map/all_gather | solution.py:90
  7.9 67.9 %all-gather.5.cloned.1.call-start = ((), (), s32[]{:S(2)}) async-start(), calls=%async_computation.1 | async-start | bytes 3932160 | tf_op jit(solution)/shard_map/all_gather | solution.py:91
  8.7 245.9 %all-reduce.7.cloned.1.call-start = ((), (), s32[]{:S(2)}) async-start(), calls=%async_computation.2 | async-start | bytes 278528 | tf_op jit(solution)/shard_map/psum | solution.py:155
  8.9 14.7 %copy-start.8 = (f32[512]{0:T(512)S(1)}, f32[512]{0:T(512)}, u32[]{:S(2)}) copy-start(f32[512]{0:T(512)} %param.17) | copy-start | bytes 6148
  8.9 14.7 %copy-start.9 = (f32[512]{0:T(512)S(1)}, f32[512]{0:T(512)}, u32[]{:S(2)}) copy-start(f32[512]{0:T(512)} %param.16) | copy-start | bytes 6148
  25.3 7.0 %copy-start.3 = (bf16[12,1,16,768]{3,2,1,0:T(8,128)(2,1)S(1)}, bf16[12,1,16,768]{3,2,1,0:T(8,128)(2,1)}, u32[]{:S(2)}) copy-start(bf16[12,1,16,768]{3,2,1,0:T(8,128)(2,1)} %param.25) | copy-start | bytes 884740
  27.4 35.9 %collective-permute-start.1 = (f32[12,1,32,4]{2,3,1,0:T(4,128)S(1)}, f32[12,1,32,4]{2,3,1,0:T(4,128)S(1)}, u32[]{:S(2)}, u32[]{:S(2)}) collective-permute-start(f32[12,1,32,4]{2,3,1,0:T(4,128)S(1)} %get-tuple-element.42), channel_id=1, source_target_pairs={{8,0},{16,8},{24,16},{9,1},{17,9},{25,17},{10,2},{18,10},{26,18},{... | collective-permute-start | bytes 18440 | tf_op jit(solution)/shard_map/ppermute | solution.py:22
  28.7 33.8 %collective-permute-start = (f32[12,1,32,4]{2,3,1,0:T(4,128)}, f32[12,1,32,4]{2,3,1,0:T(4,128)}, u32[]{:S(2)}, u32[]{:S(2)}) collective-permute-start(f32[12,1,32,4]{2,3,1,0:T(4,128)} %get-tuple-element.43), channel_id=1, source_target_pairs={{0,8},{8,16},{16,24},{1,9},{9,17},{17,25},{2,10},{10,18},{18,26},{... | collective-permute-start | bytes 18440 | tf_op jit(solution)/shard_map/ppermute | solution.py:19
  54.7 9.0 %copy-start.7 = (f32[1024]{0:T(1024)S(1)}, f32[1024]{0:T(1024)}, u32[]{:S(2)}) copy-start(f32[1024]{0:T(1024)} %param.20) | copy-start | bytes 12292
  54.7 9.9 %copy-start.6 = (f32[2048]{0:T(1024)S(1)}, f32[2048]{0:T(1024)}, u32[]{:S(2)}) copy-start(f32[2048]{0:T(1024)} %param.22) | copy-start | bytes 24580
  64.6 11.3 %copy-start.10 = (f32[768]{0:T(1024)S(1)}, f32[768]{0:T(1024)}, u32[]{:S(2)}) copy-start(f32[768]{0:T(1024)} %param.24) | copy-start | bytes 9220
  68.9 10.3 %copy-start.2 = (f32[192,768]{1,0:T(8,128)S(1)}, f32[192,768]{1,0:T(8,128)}, u32[]{:S(2)}) copy-start(f32[192,768]{1,0:T(8,128)} %bitcast_multiply_fusion.1) | copy-start | bytes 1769476
  79.3 0.8 copy-start.4
  87.5 4.8 %collective-permute-start.2 = (bf16[12,1,32,4]{0,2,3,1:T(8,128)(2,1)S(1)}, bf16[12,1,32,4]{0,2,3,1:T(8,128)(2,1)S(1)}, u32[]{:S(2)}, u32[]{:S(2)}) collective-permute-start(bf16[12,1,32,4]{0,2,3,1:T(8,128)(2,1)S(1)} %get-tuple-element.44), channel_id=1, source_target_pairs={{0,8},{8,16},{16,24},{1,9},{9,17},{17,25},{2,10},{10,18},{18,26},{... | collective-permute-start | bytes 9224 | tf_op jit(solution)/shard_map/ppermute | solution.py:19
  89.7 3.1 %collective-permute-start.3 = (bf16[12,1,32,4]{0,2,3,1:T(8,128)(2,1)S(1)}, bf16[12,1,32,4]{0,2,3,1:T(8,128)(2,1)S(1)}, u32[]{:S(2)}, u32[]{:S(2)}) collective-permute-start(bf16[12,1,32,4]{0,2,3,1:T(8,128)(2,1)S(1)} %get-tuple-element.45), channel_id=1, source_target_pairs={{8,0},{16,8},{24,16},{9,1},{17,9},{25,17},{10,2},{18,10},{26,18},{... | collective-permute-start | bytes 9224 | tf_op jit(solution)/shard_map/ppermute | solution.py:22
Sparse Core Ops, SparseCore 0:
  9.6 36.0 all-gather.2
  47.2 28.5 all-gather.4
  128.4 126.0 all-reduce.6
where the time goes:
time: 265 us; the launch traced here: 264 us
  waiting for transfers between devices  93.4 us (35%)
  blocking collectives  66.2 us (25%)
  local copies, waits for them, and re-layouts  48 us (18%)
  matrix products  21.2 us (8%)
  between operations  14.2 us (5%)
  other arithmetic  12.5 us (5%)
  starting transfers between devices  8.67 us (3%)
    psum x1, waiting for transfers between devices, shards(): lax.psum((conv_part, gain_part, bias_part, embed_part), ('rows', 'batch'))  84.6 us
    psum x1, blocking collectives, shards(): lax.psum((conv_part, gain_part, bias_part, embed_part), ('rows', 'batch'))  40.3 us
    reshape x2, local copies, waits for them, and re-layouts, shards(): grouped = values.reshape(images, height * across, GROUPS, per_group)  14 us
    psum x1, blocking collectives, shards(): lax.psum((jnp.sum(grad_norm, axis=(1, 3)), jnp.sum(grad_norm * normed_gro...  12.6 us
    unnamed x31, local copies, waits for them, and re-layouts  8.16 us
    sub x5, local copies, waits for them, and re-layouts, shards(): centred = grouped - (totals / members)[:, None, :, None]  7.65 us
    mul x5, local copies, waits for them, and re-layouts, shards(): inverse * (grad_norm - (first / members)[:, None, :, None] - normed_group...  7.62 us
    psum x1, blocking collectives, shards(): totals = lax.psum(jnp.sum(grouped, axis=(1, 3)), 'rows')  7.05 us
  transfers between devices with their start and end apart: 7, of which 3 were waited for; matrix products, arithmetic and copies ran while one was open for 17% of the time, Pallas kernels for 0%

commit v1 on v0

--- a/solution.py
+++ b/solution.py
@@ -9,6 +9,11 @@
 ALIGN = 768
 EPS_NORM = 1e-06
 EPS_UNIT = 1e-06
+
+
+def by_each_axis(array, inner_axis, outer_axis):
+    inner = lax.psum(array, inner_axis)
+    return lax.psum(inner, outer_axis)
 
 
 def padded(block, sides, width):
@@ -152,8 +157,8 @@
         - normed_groups * (second / members)[:, None, :, None]
     )
     grad_features = grad_values.reshape(images, height, across, channels).astype(jnp.bfloat16)
-    grad_conv, grad_gain, grad_bias, grad_embed = lax.psum(
-        (conv_part, gain_part, bias_part, embed_part), ("rows", "batch")
+    grad_conv, grad_gain, grad_bias, grad_embed = by_each_axis(
+        (conv_part, gain_part, bias_part, embed_part), "batch", "rows"
     )
     return (grad_features, grad_conv, grad_gain, grad_bias, grad_embed)
 

time: 265 us -> 232 us (0.88)
  blocking collectives: 66.2 us -> 43.3 us
  waiting for transfers between devices: 93.4 us -> 81.8 us
    psum x1, blocking collectives: 40.3 us -> 18.6 us  [by_each_axis(): inner = lax.psum(array, inner_axis)]
    psum x1 -> x2, waiting for transfers between devices: 84.6 us -> 73 us  [the longest x1 41.8 us: by_each_axis(): inner = lax.psum(array, inner_axis)]
  transfers between devices with their start and end apart: 7 -> 8, of which waited for: 3 -> 4; matrix products, arithmetic and copies ran while one was open for 17% -> 19% of each run, Pallas kernels for 0% -> 0%
where the time goes in v1:
time: 232 us; the launch traced here: 230 us
  waiting for transfers between devices  81.8 us (35%)
  local copies, waits for them, and re-layouts  48 us (21%)
  blocking collectives  43.3 us (19%)
  matrix products  21.2 us (9%)
  between operations  14.2 us (6%)
  other arithmetic  12.5 us (5%)
  starting transfers between devices  8.72 us (4%)
    psum x1, waiting for transfers between devices, by_each_axis(): inner = lax.psum(array, inner_axis)  41.8 us
    psum x1, waiting for transfers between devices, by_each_axis(): return lax.psum(inner, outer_axis)  31.1 us
    psum x1, blocking collectives, by_each_axis(): inner = lax.psum(array, inner_axis)  18.6 us
    reshape x2, local copies, waits for them, and re-layouts, shards(): grouped = values.reshape(images, height * across, GROUPS, per_group)  14 us
    psum x1, blocking collectives, shards(): lax.psum((jnp.sum(grad_norm, axis=(1, 3)), jnp.sum(grad_norm * normed_gro...  11.4 us
    unnamed x31, local copies, waits for them, and re-layouts  8.16 us
    sub x5, local copies, waits for them, and re-layouts, shards(): centred = grouped - (totals / members)[:, None, :, None]  7.65 us
    mul x5, local copies, waits for them, and re-layouts, shards(): inverse * (grad_norm - (first / members)[:, None, :, None] - normed_group...  7.62 us
  transfers between devices with their start and end apart: 8, of which 4 were waited for; matrix products, arithmetic and copies ran while one was open for 19% of the time, Pallas kernels for 0%

profile of v1, /device:TPU:8, one launch (start us, length us, event | category | flops | bytes accessed | tf_op | source)
XLA Modules:
  0.0 229.6 jit_solution(9858763514412575561)
XLA Ops:
  7.2 0.7 all-gather.3.cloned.1.call-update
  8.0 0.7 all-gather.5.cloned.1.call-update
  8.9 0.2 convert_reduce_fusion
  9.3 7.0 %psum.84 = f32[12,32]{1,0:T(8,128)S(1)} all-reduce(f32[12,32]{1,0:T(8,128)S(1)} %reduce_sum.97), channel_id=1, replica_groups=mesh['rows'=4,'batch'=8] {'rows'}, use_global_device_ids=true, to_apply=%region_2.0 | all-reduce | flops 384 | bytes 3072 | tf_op jit(solution)/shard_map/psum | solution.py:56
  16.5 0.1 sub.51
  16.6 0.2 multiply_reduce_fusion.1
  17.1 6.2 %psum.85 = f32[12,32]{1,0:T(8,128)S(1)} all-reduce(f32[12,32]{1,0:T(8,128)S(1)} %reduce_sum.100), channel_id=1, replica_groups=mesh['rows'=4,'batch'=8] {'rows'}, use_global_device_ids=true, to_apply=%region_5.6 | all-reduce | flops 384 | bytes 3072 | tf_op jit(solution)/shard_map/psum | solution.py:58
  23.5 0.1 mul.137
  23.6 1.7 multiply_convert_fusion.2
  25.3 0.8 fusion.12
  26.1 0.7 fusion.35
  26.8 0.6 fusion.47
  27.4 1.3 collective-permute-start.1
  28.7 3.6 %collective-permute-start = (f32[12,1,32,4]{2,3,1,0:T(4,128)}, f32[12,1,32,4]{2,3,1,0:T(4,128)}, u32[]{:S(2)}, u32[]{:S(2)}) collective-permute-start(f32[12,1,32,4]{2,3,1,0:T(4,128)} %get-tuple-element.47), channel_id=1, source_target_pairs={{0,8},{8,16},{16,24},{1,9},{9,17},{17,25},{2,10},{10,18},{18,26},{... | collective-permute-start | bytes 18440 | tf_op jit(solution)/shard_map/ppermute | solution.py:24
  32.5 0.9 bitcast_multiply_fusion.1
  33.7 6.2 %copy.155 = f32[12,2,32,512]{2,1,0,3:T(2,128)} copy(bf16[12,2,32,512]{3,2,1,0:T(8,128)(2,1)S(1)} %copy-done.1) | data formatting | bytes 2359296 | tf_op jit(solution)/shard_map/reshape | solution.py:55
  39.9 2.4 %mul.163 = f32[12,64,32,16]{1,0,3,2:T(8,128)} broadcast(f32[12,32]{0,1:T(8,128)S(1)} %copy.146), dimensions={0,2} | broadcast | bytes 1574400 | tf_op jit(solution)/shard_map/mul | solution.py:154
  42.3 3.4 %mul.171 = f32[768,512]{0,1:T(8,128)S(1)} reshape(f32[12,64,32,16]{1,0,3,2:T(8,128)} %mul.163) | data formatting | bytes 3145728 | tf_op jit(solution)/shard_map/mul | solution.py:154
  45.7 1.6 copy.150
  47.3 2.4 %sub.61 = f32[12,64,32,16]{1,0,3,2:T(8,128)} broadcast(f32[12,32]{0,1:T(8,128)S(1)} %copy.144), dimensions={0,2} | broadcast | bytes 1574400 | tf_op jit(solution)/shard_map/sub | solution.py:57
  49.7 3.3 %sub.64 = f32[768,512]{0,1:T(8,128)S(1)} reshape(f32[12,64,32,16]{1,0,3,2:T(8,128)} %sub.61) | data formatting | bytes 3145728 | tf_op jit(solution)/shard_map/sub | solution.py:57
  53.1 1.6 copy.149
  54.7 7.8 %reshape.201 = f32[12,64,32,16]{1,0,3,2:T(8,128)} reshape(f32[12,2,32,512]{2,1,0,3:T(2,128)} %copy.155) | data formatting | bytes 3145728 | tf_op jit(solution)/shard_map/reshape | solution.py:55
  62.5 0.8 fusion.41
  63.4 0.2 copy.138
  63.7 0.8 fusion.10
  64.6 4.3 %convolution_add_fusion = f32[192,2048]{1,0:T(8,128)} fusion(bf16[192,1024]{1,0:T(8,128)(2,1)S(1)} %fusion.10, bf16[1024,2048]{1,0:T(8,128)(2,1)} %all-gather.3.cloned.1.call-done, f32[2048]{0:T(1024)S(1)} %copy-done.6), kind=kOutput, calls=%fused_computation.11 | convolution fusion | flops 805699584 | bytes 6168576 | tf_op jit(solution)/shard_map/dot_general | solution.py:98
  68.9 6.9 %all-gather.5.cloned.1.call-done = bf16[2048,768]{1,0:T(8,128)(2,1)} async-done(((bf16[512,768]{1,0:T(8,128)(2,1)}), bf16[2048,768]{1,0:T(8,128)(2,1)}) %all-gather.5.cloned.1.call-update) | async-done | bytes 3145744 | tf_op jit(solution)/shard_map/all_gather | solution.py:96
  75.8 3.4 %multiply_reduce_fusion.4 = (f32[192]{0:T(256)S(1)}, f32[192,768]{1,0:T(8,128)S(1)}) fusion(f32[768]{0:T(1024)S(1)} %copy-done.10, bf16[2048,768]{1,0:T(8,128)(2,1)} %all-gather.5.cloned.1.call-done, f32[192,2048]{1,0:T(8,128)} %convolution_add_fusion), kind=kOutput, calls=%fused_computation.47 | convolution fusion | flops 606388032 | bytes 5312256 | tf_op jit(solution)/shard_map/dot_general | solution.py:100
  79.3 0.2 multiply_reduce_fusion.2
  79.5 0.5 copy-done.4
  80.1 6.4 %fusion.11 = f32[192,1024]{1,0:T(8,128)S(1)} fusion(bf16[1024,2048]{1,0:T(8,128)(2,1)} %all-gather.3.cloned.1.call-done, bf16[2048,768]{1,0:T(8,128)(2,1)} %all-gather.5.cloned.1.call-done, f32[192,2048]{1,0:T(8,128)} %convolution_add_fusion, f32[192,768]{1,0:T(8,128)S(1)} %copy-done.2, f32[192,768]{1,0:T(8,128)} %copy-done.4, ...), kind=kOutput, calls=%fused_computation.37 | convolution fusion | flops 1413562368 | bytes 10881280 | tf_op jit(solution)/shard_map/dot_general | solution.py:111
  86.5 0.7 convolution_convert_fusion
  87.3 0.2 copy.139
  87.5 2.1 collective-permute-start.2
  89.7 1.5 collective-permute-start.3
  91.2 1.1 fusion.49
  92.3 0.5 collective-permute-done.3
  92.8 0.7 slice_dynamic-update-slice_fusion.5
  93.5 0.6 fusion.38
  94.1 0.6 slice_dynamic-update-slice_fusion.4
  94.8 0.7 slice_dynamic-update-slice_fusion.3
  95.4 0.6 constant_dynamic-update-slice_fusion
  96.1 0.6 slice_dynamic-update-slice_fusion.2
  96.7 0.7 slice_dynamic-update-slice_fusion.1
  97.4 0.6 fusion.37
  98.0 0.6 slice_dynamic-update-slice_fusion
  98.6 1.6 copy.140
  100.2 0.2 reshape.185
  100.4 0.3 convolution_bitcast_fusion
  100.7 0.7 copy.157
  101.4 3.3 %fusion.46 = (f32[512]{0:T(512)S(1)}, f32[512]{0:T(512)S(1)}, f32[768,512]{1,0:T(8,128)S(1)}) fusion(f32[768,512]{1,0:T(8,128)} %copy.150, f32[768,512]{1,0:T(8,128)} %copy.149, bf16[12,2,32,512]{3,2,1,0:T(8,128)(2,1)S(1)} %copy-done.1, f32[512]{0:T(512)S(1)} %copy-done.9, f32[12,2,32,512]{3,2,1,0:T(8,128)} %get-tuple-element.45, ...), kind=kOutput, calls=%fused_computation.94 | convolution fusion | flops 34208768 | bytes 7176192 | tf_op jit(solution)/shard_map/dot_general | solution.py:141
  104.7 1.6 copy.141
  106.3 4.0 %reshape.188 = f32[12,64,32,16]{1,0,3,2:T(8,128)} reshape(f32[768,512]{0,1:T(8,128)} %copy.141) | data formatting | bytes 3145728 | tf_op jit(solution)/shard_map/reshape | solution.py:149
  110.3 4.7 %fusion.45 = (f32[12,32]{0,1:T(8,128)S(1)}, f32[12,32]{0,1:T(8,128)S(1)}) fusion(f32[12,64,32,16]{1,0,3,2:T(8,128)} %reshape.188, f32[12,32]{0,1:T(8,128)S(1)} %copy.146, f32[12,64,32,16]{1,0,3,2:T(8,128)} %reshape.201, f32[12,32]{0,1:T(8,128)S(1)} %copy.144), kind=kLoop, calls=%fused_computation.93 | loop fusion | flops 1965312 | bytes 3151872 | tf_op jit(solution)/shard_map/reduce_sum | solution.py:152
  115.3 18.6 %all-reduce.2 = (f32[512]{0:T(512)S(1)}, f32[512]{0:T(512)S(1)}) all-reduce(f32[512]{0:T(512)S(1)} %get-tuple-element.32, f32[512]{0:T(512)S(1)} %get-tuple-element.31), channel_id=1, replica_groups=mesh['rows'=4,'batch'=8] {'batch'}, use_global_device_ids=true, to_apply=%region_16.17 | all-reduce | flops 1024 | bytes 8192 | tf_op jit(solution)/shard_map/psum | solution.py:15
  133.9 11.4 %all-reduce.4 = (f32[12,32]{1,0:T(8,128)S(1)}, f32[12,32]{1,0:T(8,128)S(1)}, f32[512]{0:T(512)}, f32[512]{0:T(512)}) all-reduce(f32[12,32]{1,0:T(8,128)S(1)} %copy.147, f32[12,32]{1,0:T(8,128)S(1)} %copy.142, f32[512]{0:T(512)S(1)} %get-tuple-element.33, f32[512]{0:T(512)S(1)} %get-tuple-element.34), channel_id=1, replica_groups=mesh['rows'=4,'batch'=8] {'rows'}, use_global_device_ids=true, to_apply=%region_12.13 | all-reduce | flops 1792 | bytes 14336 | tf_op jit(solution)/shard_map/psum | solution.py:151
  145.4 0.1 mul.167
  145.7 0.1 sub.58
  145.8 41.8 %all-reduce.9.cloned.1.call-done = (f32[4,4608]{1,0:T(4,128)}, f32[16,1024]{1,0:T(8,128)}) async-done(((f32[4,4608]{1,0:T(4,128)}, f32[16,1024]{1,0:T(8,128)}), (f32[4,4608]{1,0:T(4,128)}, f32[16,1024]{1,0:T(8,128)})) %all-reduce.9.cloned.1.call-update) | async-done | bytes 139280 | tf_op jit(solution)/shard_map/psum | solution.py:15
  187.6 1.3 multiply_convert_fusion
  189.0 31.1 %all-reduce.11.cloned.1.call-done = (f32[4,4608]{1,0:T(4,128)}, f32[16,1024]{1,0:T(8,128)}) async-done(((f32[4,4608]{1,0:T(4,128)}, f32[16,1024]{1,0:T(8,128)}), (f32[4,4608]{1,0:T(4,128)}, f32[16,1024]{1,0:T(8,128)})) %all-reduce.11.cloned.1.call-update) | async-done | bytes 139280 | tf_op jit(solution)/shard_map/psum | solution.py:16
  220.1 1.5 copy.176
  221.6 1.5 copy.177
  (62 shorter events, 2.3 us)
Async XLA Ops:
  7.2 56.6 %copy-start = (f32[16,1024]{1,0:T(8,128)S(1)}, f32[16,1024]{1,0:T(8,128)}, u32[]{:S(2)}) copy-start(f32[16,1024]{1,0:T(8,128)} %param.19) | copy-start | bytes 196612
  7.2 1.6 copy-start.5
  7.2 1.7 copy-start.1
  7.2 57.4 %all-gather.3.cloned.1.call-start = ((), (), s32[]{:S(2)}) async-start(), calls=%async_computation | async-start | bytes 5242880 | tf_op jit(solution)/shard_map/all_gather | solution.py:95
  7.9 67.9 %all-gather.5.cloned.1.call-start = ((), (), s32[]{:S(2)}) async-start(), calls=%async_computation.1 | async-start | bytes 3932160 | tf_op jit(solution)/shard_map/all_gather | solution.py:96
  8.7 178.9 %all-reduce.9.cloned.1.call-start = ((), (), s32[]{:S(2)}) async-start(), calls=%async_computation.2 | async-start | bytes 278528 | tf_op jit(solution)/shard_map/psum | solution.py:15
  8.9 14.7 %copy-start.8 = (f32[512]{0:T(512)S(1)}, f32[512]{0:T(512)}, u32[]{:S(2)}) copy-start(f32[512]{0:T(512)} %param.17) | copy-start | bytes 6148
  8.9 14.7 %copy-start.9 = (f32[512]{0:T(512)S(1)}, f32[512]{0:T(512)}, u32[]{:S(2)}) copy-start(f32[512]{0:T(512)} %param.16) | copy-start | bytes 6148
  25.3 7.0 %copy-start.3 = (bf16[12,1,16,768]{3,2,1,0:T(8,128)(2,1)S(1)}, bf16[12,1,16,768]{3,2,1,0:T(8,128)(2,1)}, u32[]{:S(2)}) copy-start(bf16[12,1,16,768]{3,2,1,0:T(8,128)(2,1)} %param.25) | copy-start | bytes 884740
  27.4 35.9 %collective-permute-start.1 = (f32[12,1,32,4]{2,3,1,0:T(4,128)S(1)}, f32[12,1,32,4]{2,3,1,0:T(4,128)S(1)}, u32[]{:S(2)}, u32[]{:S(2)}) collective-permute-start(f32[12,1,32,4]{2,3,1,0:T(4,128)S(1)} %get-tuple-element.46), channel_id=1, source_target_pairs={{8,0},{16,8},{24,16},{9,1},{17,9},{25,17},{10,2},{18,10},{26,18},{... | collective-permute-start | bytes 18440 | tf_op jit(solution)/shard_map/ppermute | solution.py:27
  28.7 33.8 %collective-permute-start = (f32[12,1,32,4]{2,3,1,0:T(4,128)}, f32[12,1,32,4]{2,3,1,0:T(4,128)}, u32[]{:S(2)}, u32[]{:S(2)}) collective-permute-start(f32[12,1,32,4]{2,3,1,0:T(4,128)} %get-tuple-element.47), channel_id=1, source_target_pairs={{0,8},{8,16},{16,24},{1,9},{9,17},{17,25},{2,10},{10,18},{18,26},{... | collective-permute-start | bytes 18440 | tf_op jit(solution)/shard_map/ppermute | solution.py:24
  54.7 9.0 %copy-start.7 = (f32[1024]{0:T(1024)S(1)}, f32[1024]{0:T(1024)}, u32[]{:S(2)}) copy-start(f32[1024]{0:T(1024)} %param.20) | copy-start | bytes 12292
  54.7 9.9 %copy-start.6 = (f32[2048]{0:T(1024)S(1)}, f32[2048]{0:T(1024)}, u32[]{:S(2)}) copy-start(f32[2048]{0:T(1024)} %param.22) | copy-start | bytes 24580
  64.6 11.3 %copy-start.10 = (f32[768]{0:T(1024)S(1)}, f32[768]{0:T(1024)}, u32[]{:S(2)}) copy-start(f32[768]{0:T(1024)} %param.24) | copy-start | bytes 9220
  68.9 10.3 %copy-start.2 = (f32[192,768]{1,0:T(8,128)S(1)}, f32[192,768]{1,0:T(8,128)}, u32[]{:S(2)}) copy-start(f32[192,768]{1,0:T(8,128)} %bitcast_multiply_fusion.1) | copy-start | bytes 1769476
  79.3 0.8 copy-start.4
  87.5 4.8 %collective-permute-start.2 = (bf16[12,1,32,4]{0,2,3,1:T(8,128)(2,1)S(1)}, bf16[12,1,32,4]{0,2,3,1:T(8,128)(2,1)S(1)}, u32[]{:S(2)}, u32[]{:S(2)}) collective-permute-start(bf16[12,1,32,4]{0,2,3,1:T(8,128)(2,1)S(1)} %get-tuple-element.48), channel_id=1, source_target_pairs={{0,8},{8,16},{16,24},{1,9},{9,17},{17,25},{2,10},{10,18},{18,26},{... | collective-permute-start | bytes 9224 | tf_op jit(solution)/shard_map/ppermute | solution.py:24
  89.7 3.1 %collective-permute-start.3 = (bf16[12,1,32,4]{0,2,3,1:T(8,128)(2,1)S(1)}, bf16[12,1,32,4]{0,2,3,1:T(8,128)(2,1)S(1)}, u32[]{:S(2)}, u32[]{:S(2)}) collective-permute-start(bf16[12,1,32,4]{0,2,3,1:T(8,128)(2,1)S(1)} %get-tuple-element.49), channel_id=1, source_target_pairs={{8,0},{16,8},{24,16},{9,1},{17,9},{25,17},{10,2},{18,10},{26,18},{... | collective-permute-start | bytes 9224 | tf_op jit(solution)/shard_map/ppermute | solution.py:27
  115.2 104.9 %all-reduce.11.cloned.1.call-start = ((), (), s32[]{:S(2)}) async-start(), calls=%async_computation.3 | async-start | bytes 278528 | tf_op jit(solution)/shard_map/psum | solution.py:16
Sparse Core Ops, SparseCore 0:
  9.6 36.0 all-gather.2
  47.2 28.5 all-gather.4
  115.3 72.2 all-reduce.8
  189.9 30.1 all-reduce.10
